TPU v7x, 512 devices: a whole 4x4x16 slice. The times are simulated.
512 devices in a mesh: row: 16 (over z_hi, y), col: 4 (over x), cuts: 8 (over z_lo, core).
Axes of the slice: x: 4, y: 4, z: 16 (z_hi: 4, z_lo: 4; z = z_hi * 4 + z_lo), core: 2. Of those that a mesh axis runs over, the one named last changes fastest.
Arguments:
- warm: float32 [40, 131072], P('cuts', ('row', 'col')), may hold values from -6 to 6
- tiles: float32 [22016, 128, 128], P(('row', 'col', 'cuts')), may hold values from -0.125 to 0.125
- tile_rows: int32 [22016], P(('row', 'col', 'cuts')), may hold values from -1 to 1023, as said below
- tile_cols: int32 [22016], P(('row', 'col', 'cuts')), may hold values from 0 to 1023, as said below
Outputs:
- basis: float32 [40, 131072], P('cuts', ('row', 'col'))
- residual: float32 [40, 131072], P('cuts', ('row', 'col'))
Inputs may be any that keep to these rules, and one draw needn't show every extreme that they name: `tile_rows`: slots come in groups of 344; group r * (size of col) + c belongs to the grid position with row index r and column index c. A group's tiles lie in the block rows r * (size of col) * 16 up to (r + 1) * (size of col) * 16 - 1, and in block columns j with (j // 16) % (size of col) = c. No block appears twice. In each group the live slots come first and fill at least half of it; some group is full. Block rows hold uneven numbers of tiles. `tile_cols`: see tile_rows; an empty slot's column is that of some block the group may hold.
All inputs are finite; a program needn't handle non-finite values.
Results may differ from a plain program's by a relative error of at most 0.0003.
Values sent between devices are 32-bit elements; how exact they have to be, the bound alone decides.
A program may use at most 64 MiB of HBM per device.

v0:
```python
import jax
import jax.numpy as jnp
from jax import lax
from jax.sharding import PartitionSpec as P


def copy_for_each(shard, axis):
    devices = lax.axis_size(axis)
    return lax.all_to_all(
        jnp.broadcast_to(shard[None], (devices, *shard.shape)), axis, 0, 0, tiled=True
    )


def in_order(parts, dim):
    dims = list(parts.shape[1:])
    dims[dim] *= parts.shape[0]
    return jnp.moveaxis(parts, 0, dim).reshape(dims)


def collect(shard, axis, dim):
    parts = copy_for_each(shard, axis)
    return in_order(parts, dim)


def in_blocks(shard, dim, devices):
    dims = shard.shape
    parts = shard.reshape(*dims[:dim], devices, dims[dim] // devices, *dims[dim + 1 :])
    return jnp.moveaxis(parts, dim, 0)


def summed_on_arrival(shard, axis, dim):
    parts = in_blocks(shard, dim, lax.axis_size(axis))
    arrived = lax.all_to_all(parts, axis, split_axis=0, concat_axis=0, tiled=True)
    return arrived.sum(axis=0)


def over_copies(shard, axis):
    everything = copy_for_each(shard, axis)
    return jnp.sum(everything, axis=0)


def block_product(panel, tiles, rows, positions, base, out_blocks):
    count_rows = panel.shape[0]
    block = tiles.shape[1]
    blocks = panel.reshape(count_rows, -1, block)
    picked = jnp.take(blocks, positions, axis=1)
    prods = jnp.einsum("suv,ksv->ksu", tiles, picked, precision=lax.Precision.HIGHEST)
    local = rows - base
    onehot = (local[:, None] == jnp.arange(out_blocks, dtype=jnp.int32)[None, :]).astype(
        jnp.float32
    )
    summed = jnp.einsum("ksu,sb->kbu", prods, onehot, precision=lax.Precision.HIGHEST)
    return summed.reshape(count_rows, out_blocks * block)


def operator_apply(vectors, tiles, rows, positions, base, out_blocks):
    panel = collect(vectors, "cuts", 0)
    panel = lax.all_gather(panel, "row", axis=1, tiled=True)
    partial_value = block_product(panel, tiles, rows, positions, base, out_blocks)
    partial_value = summed_on_arrival(partial_value, "col", 1)
    return summed_on_arrival(partial_value, "cuts", 0)


def shards(warm, tiles, tile_rows, tile_cols):
    ncol = lax.axis_size("col")
    nrow = lax.axis_size("row")
    block = tiles.shape[1]
    seg_blocks = warm.shape[1] // block
    out_blocks = ncol * seg_blocks
    items = warm.shape[1] * nrow * ncol
    base = lax.axis_index("row") * out_blocks
    segment = tile_cols // seg_blocks
    positions = segment // ncol * seg_blocks + tile_cols % seg_blocks
    image = operator_apply(warm, tiles, tile_rows, positions, base, out_blocks)
    whole = collect(image, "cuts", 0)
    local_gram = jnp.dot(
        whole, whole.T, precision=lax.Precision.HIGHEST, preferred_element_type=jnp.float32
    )
    gram = over_copies(local_gram, ("row", "col")) / items
    lower = jnp.linalg.cholesky(gram)
    kloc = warm.shape[0]
    start = lax.axis_index("cuts") * kloc
    inverse = lax.linalg.triangular_solve(
        lower, jnp.eye(whole.shape[0], dtype=jnp.float32), left_side=True, lower=True
    )
    mine_rows = lax.dynamic_slice_in_dim(inverse, start, kloc, 0)
    basis = jnp.dot(
        mine_rows, whole, precision=lax.Precision.HIGHEST, preferred_element_type=jnp.float32
    )
    basis_all = collect(basis, "cuts", 0)
    product = operator_apply(basis, tiles, tile_rows, positions, base, out_blocks)
    local_projection = jnp.dot(
        basis_all, product.T, precision=lax.Precision.HIGHEST, preferred_element_type=jnp.float32
    )
    projected = over_copies(local_projection, ("row", "col")) / items
    residual = product - jnp.dot(
        projected.T, basis_all, precision=lax.Precision.HIGHEST, preferred_element_type=jnp.float32
    )
    return (basis, residual)


def solution(mesh):
    return jax.shard_map(
        shards,
        mesh=mesh,
        in_specs=(
            P("cuts", ("row", "col")),
            P(("row", "col", "cuts"), None, None),
            P(("row", "col", "cuts")),
            P(("row", "col", "cuts")),
        ),
        out_specs=(P("cuts", ("row", "col")), P("cuts", ("row", "col"))),
        check_vma=False,
    )
```

profile of v0, /device:TPU:1, one launch (start us, length us, event | category | flops | bytes accessed | tf_op | source)
XLA Modules:
  0.0 604.3 jit_solution(9353652540865754813)
XLA Ops:
  8.3 23.5 %all_to_all.46 = f32[8,5,2048]{2,1,0:T(8,128)S(1)} all-to-all(f32[8,5,2048]{2,1,0:T(8,128)S(1)} %broadcast_in_dim.20), channel_id=1, replica_groups=mesh['row'=16,'col'=4,'cuts'=8] {'cuts'}, dimensions={0} | all-to-all | bytes 655360 | tf_op jit(solution)/shard_map/all_to_all | solution.py:9
  32.7 155.9 %all-gather.3.cloned.1.call-done = f32[40,32768]{1,0:T(8,128)} async-done(((f32[40,2048]{1,0:T(8,128)}), f32[40,32768]{1,0:T(8,128)}) %all-gather.3.cloned.1.call-update) | async-done | bytes 5242896 | tf_op jit(solution)/shard_map/all_gather | solution.py:58
  188.6 5.2 copy_bitcast_fusion.1
  193.8 4.0 gather_fusion
  197.8 6.9 %convolution_bitcast_fusion.3 = f32[40,43,128]{2,0,1:T(8,128)S(1)} fusion(f32[43,128,128]{2,1,0:T(8,128)S(1)} %copy-done, f32[43,40,128]{2,1,0:T(8,128)} %gather_fusion, pred[43]{0:T(512)(128)(4,1)S(1)} %get-tuple-element.3), kind=kOutput, calls=%fused_computation.8 | convolution fusion | flops 338385920 | bytes 4579371 | tf_op jit(solution)/shard_map/suv,ksv->ksu/dot_general | solution.py:47
  204.6 1.9 convolution_bitcast_fusion.1
  206.5 2.7 reshape_reshape.6
  209.2 2.1 copy.55
  211.2 20.7 %all_to_all.47 = f32[4,40,2048]{2,1,0:T(8,128)} all-to-all(f32[4,40,2048]{2,1,0:T(8,128)S(1)} %bitcast.55), channel_id=1, replica_groups=mesh['row'=16,'col'=4,'cuts'=8] {'col'}, dimensions={0} | all-to-all | bytes 2621440 | tf_op jit(solution)/shard_map/all_to_all | solution.py:33
  232.0 2.2 reduce_sum.56
  235.1 19.3 %all_to_all.48 = f32[8,5,2048]{2,1,0:T(8,128)} all-to-all(f32[8,5,2048]{2,1,0:T(8,128)S(1)} %reshape.48), channel_id=1, replica_groups=mesh['row'=16,'col'=4,'cuts'=8] {'cuts'}, dimensions={0} | all-to-all | bytes 655360 | tf_op jit(solution)/shard_map/all_to_all | solution.py:33
  255.6 18.4 %all_to_all.49 = f32[8,5,2048]{2,1,0:T(8,128)} all-to-all(f32[8,5,2048]{2,1,0:T(8,128)S(1)} %broadcast_in_dim.22), channel_id=1, replica_groups=mesh['row'=16,'col'=4,'cuts'=8] {'cuts'}, dimensions={0} | all-to-all | bytes 655360 | tf_op jit(solution)/shard_map/all_to_all | solution.py:9
  276.6 3.2 reshape.76
  279.8 10.5 %all-to-all-start.4 = ((f32[64,1,1600]{2,1,0:T(1,128)}), f32[64,1,1600]{2,1,0:T(1,128)}, u32[]{:S(2)}, u32[]{:S(2)}) async-start(f32[64,1,1600]{2,1,0:T(1,128)} %reshape.76), calls=%async_computation.4 | async-start | bytes 851968 | tf_op jit(solution)/shard_map/all_to_all | solution.py:9
  290.5 24.7 %all-to-all-done.4 = f32[64,1,1600]{2,1,0:T(1,128)} async-done(((f32[64,1,1600]{2,1,0:T(1,128)}), f32[64,1,1600]{2,1,0:T(1,128)}, u32[]{:S(2)}, u32[]{:S(2)}) %all-to-all-start.4) | async-done | bytes 409632 | tf_op jit(solution)/shard_map/all_to_all | solution.py:9
  315.8 3.4 reduce.6
  319.2 2.6 reshape.77
  321.8 1.4 reduce_sum.58
  323.3 3.6 cholesky.17
  328.3 3.1 custom-call.6
  331.9 22.3 %all_to_all.50 = f32[8,5,2048]{2,1,0:T(8,128)S(1)} all-to-all(f32[8,5,2048]{2,1,0:T(8,128)S(1)} %broadcast_in_dim.24), channel_id=1, replica_groups=mesh['row'=16,'col'=4,'cuts'=8] {'cuts'}, dimensions={0} | all-to-all | bytes 655360 | tf_op jit(solution)/shard_map/all_to_all | solution.py:9
  355.0 146.8 %all-gather.5.cloned.1.call-done = f32[40,32768]{1,0:T(8,128)} async-done(((f32[40,2048]{1,0:T(8,128)}), f32[40,32768]{1,0:T(8,128)}) %all-gather.5.cloned.1.call-update) | async-done | bytes 5242896 | tf_op jit(solution)/shard_map/all_gather | solution.py:58
  501.9 5.1 copy_bitcast_fusion
  507.0 4.0 gather_fusion.1
  511.0 6.9 %convolution_bitcast_fusion.2 = f32[40,43,128]{2,0,1:T(8,128)S(1)} fusion(f32[43,128,128]{2,1,0:T(8,128)S(1)} %copy-done, f32[43,40,128]{2,1,0:T(8,128)} %gather_fusion.1, pred[43]{0:T(512)(128)(4,1)S(1)} %get-tuple-element.3), kind=kOutput, calls=%fused_computation.7 | convolution fusion | flops 338385920 | bytes 4579371 | tf_op jit(solution)/shard_map/suv,ksv->ksu/dot_general | solution.py:47
  517.9 1.9 convolution_bitcast_fusion
  519.8 2.7 reshape_reshape.7
  522.4 2.1 copy.54
  524.5 20.8 %all_to_all.51 = f32[4,40,2048]{2,1,0:T(8,128)} all-to-all(f32[4,40,2048]{2,1,0:T(8,128)S(1)} %bitcast.56), channel_id=1, replica_groups=mesh['row'=16,'col'=4,'cuts'=8] {'col'}, dimensions={0} | all-to-all | bytes 2621440 | tf_op jit(solution)/shard_map/all_to_all | solution.py:33
  545.4 1.4 reduce_sum.60
  547.6 20.3 %all_to_all.52 = f32[8,5,2048]{2,1,0:T(8,128)} all-to-all(f32[8,5,2048]{2,1,0:T(8,128)} %reshape.52), channel_id=1, replica_groups=mesh['row'=16,'col'=4,'cuts'=8] {'cuts'}, dimensions={0} | all-to-all | bytes 655360 | tf_op jit(solution)/shard_map/all_to_all | solution.py:33
  569.6 26.0 %all_to_all.53 = f32[64,1,200]{2,1,0:T(1,128)S(1)} all-to-all(f32[64,1,200]{2,1,0:T(1,128)S(1)} %reshape.78), channel_id=1, replica_groups=mesh['row'=16,'col'=4,'cuts'=8] {'row','col'}, dimensions={0} | all-to-all | bytes 102400 | tf_op jit(solution)/shard_map/all_to_all | solution.py:9
  (44 shorter events, 14.6 us)
Async XLA Ops:
  7.2 190.6 %copy-start = (f32[43,128,128]{2,1,0:T(8,128)S(1)}, f32[43,128,128]{2,1,0:T(8,128)}, u32[]{:S(2)}) copy-start(f32[43,128,128]{2,1,0:T(8,128)} %param.7) | copy-start | bytes 8454148
  7.2 25.4 %copy-start.3 = (s32[43]{0:T(128)S(1)}, s32[43]{0:T(128)}, u32[]{:S(2)}) copy-start(s32[43]{0:T(128)} %param.9) | copy-start | bytes 520
  7.2 25.5 %copy-start.4 = (s32[43]{0:T(128)S(1)}, s32[43]{0:T(128)}, u32[]{:S(2)}) copy-start(s32[43]{0:T(128)} %param.8) | copy-start | bytes 520
  7.2 181.4 %all-gather.3.cloned.1.call-start = ((), (), s32[]{:S(2)}) async-start(), calls=%async_computation.9 | async-start | bytes 5570560 | tf_op jit(solution)/shard_map/all_gather | solution.py:58
  279.8 35.4 %all-to-all-start.4 = ((f32[64,1,1600]{2,1,0:T(1,128)}), f32[64,1,1600]{2,1,0:T(1,128)}, u32[]{:S(2)}, u32[]{:S(2)}) async-start(f32[64,1,1600]{2,1,0:T(1,128)} %reshape.76), calls=%async_computation.4 | async-start | bytes 851968 | tf_op jit(solution)/shard_map/all_to_all | solution.py:9
  290.3 211.6 %all-gather.5.cloned.1.call-start = ((), (), s32[]{:S(2)}) async-start(), calls=%async_computation.10 | async-start | bytes 5570560 | tf_op jit(solution)/shard_map/all_gather | solution.py:58
  331.9 175.1 %copy-start.2 = (f32[5,2048]{1,0:T(8,128)}, f32[5,2048]{1,0:T(8,128)S(1)}, u32[]{:S(2)}) copy-start(f32[5,2048]{1,0:T(8,128)S(1)} %fusion.20) | copy-start | bytes 122884
  524.5 44.5 %copy-start.1 = (f32[40,2048]{1,0:T(8,128)S(1)}, f32[40,2048]{1,0:T(8,128)}, u32[]{:S(2)}) copy-start(f32[40,2048]{1,0:T(8,128)} %reshape.50) | copy-start | bytes 983044
Sparse Core Ops, SparseCore 0:
  32.7 155.8 all-gather.2
  355.2 146.6 all-gather.4
where the time goes:
time: 606 us; the launch traced here: 604 us
  waiting for transfers between devices  327 us (54%)
  blocking collectives  171 us (28%)
  local copies, waits for them, and re-layouts  41.4 us (7%)
  other arithmetic  19.6 us (3%)
  matrix products  19.6 us (3%)
  between operations  14.3 us (2%)
  starting transfers between devices  10.7 us (2%)
    all_gather x2, waiting for transfers between devices, operator_apply(): panel = lax.all_gather(panel, 'row', axis=1, tiled=True)  303 us
    all_to_all x4, blocking collectives, copy_for_each(): lax.all_to_all(jnp.broadcast_to(shard[None], (devices, *shard.shape)), ax...  90.2 us
    all_to_all x4, blocking collectives, summed_on_arrival(): lax.all_to_all(parts, axis, split_axis=0, concat_axis=0, tiled=True)  81.2 us
    all_to_all x1, waiting for transfers between devices, copy_for_each(): lax.all_to_all(jnp.broadcast_to(shard[None], (devices, *shard.shape)), ax...  24.7 us
    dot_general x2, matrix products, block_product(): jnp.einsum('suv,ksv->ksu', tiles, picked, precision=lax.Precision.HIGHEST)  13.7 us
  transfers between devices with their start and end apart: 3, of which 3 were waited for; matrix products, arithmetic and copies ran while one was open for 0% of the time, Pallas kernels for 0%

commit v1 on v0

--- a/solution.py
+++ b/solution.py
@@ -55,7 +55,9 @@
 
 def operator_apply(vectors, tiles, rows, positions, base, out_blocks):
     panel = collect(vectors, "cuts", 0)
-    panel = lax.all_gather(panel, "row", axis=1, tiled=True)
+    panel = jnp.concatenate(
+        lax.all_to_all(jnp.stack([panel] * lax.axis_size("row")), "row", 0, 0), axis=1
+    )
     partial_value = block_product(panel, tiles, rows, positions, base, out_blocks)
     partial_value = summed_on_arrival(partial_value, "col", 1)
     return summed_on_arrival(partial_value, "cuts", 0)

time: 606 us -> 813 us (1.34)
  blocking collectives: 171 us -> 407 us
  waiting for transfers between devices: 327 us -> 259 us
  local copies, waits for them, and re-layouts: 41.4 us -> 78.3 us
  starting transfers between devices: 10.7 us -> 26.9 us
  between operations: 14.3 us -> 0.85 us
    all_gather x2 -> x0, waiting for transfers between devices: 303 us -> none  [operator_apply(): panel = lax.all_gather(panel, 'row', axis=1, tiled=True)]
    all_to_all x0 -> x1, blocking collectives: none -> 237 us  [operator_apply(): lax.all_to_all(jnp.stack([panel] * lax.axis_size('row')), 'row', 0, 0)]
    all_to_all x0 -> x1, waiting for transfers between devices: none -> 234 us  [operator_apply(): lax.all_to_all(jnp.stack([panel] * lax.axis_size('row')), 'row', 0, 0)]
    another operation x0 -> x8, local copies, waits for them, and re-layouts: none -> 35.7 us  [the longest x4 29.2 us: block_product(): blocks = panel.reshape(count_rows, -1, block)]
    all_to_all x0 -> x1, starting transfers between devices: none -> 13 us  [operator_apply(): lax.all_to_all(jnp.stack([panel] * lax.axis_size('row')), 'row', 0, 0)]
  transfers between devices with their start and end apart: 3 -> 2, of which waited for: 3 -> 2; matrix products, arithmetic and copies ran while one was open for 0% -> 0% of each run, Pallas kernels for 0% -> 0%
where the time goes in v1:
time: 813 us; the launch traced here: 811 us
  blocking collectives  407 us (50%)
  waiting for transfers between devices  259 us (32%)
  local copies, waits for them, and re-layouts  78.3 us (10%)
  starting transfers between devices  26.9 us (3%)
  other arithmetic  19.6 us (2%)
  matrix products  19.6 us (2%)
    all_to_all x1, blocking collectives, operator_apply(): lax.all_to_all(jnp.stack([panel] * lax.axis_size('row')), 'row', 0, 0)  237 us
    all_to_all x1, waiting for transfers between devices, operator_apply(): lax.all_to_all(jnp.stack([panel] * lax.axis_size('row')), 'row', 0, 0)  234 us
    all_to_all x4, blocking collectives, copy_for_each(): lax.all_to_all(jnp.broadcast_to(shard[None], (devices, *shard.shape)), ax...  90 us
    all_to_all x4, blocking collectives, summed_on_arrival(): lax.all_to_all(parts, axis, split_axis=0, concat_axis=0, tiled=True)  80.6 us
    another operation x4, local copies, waits for them, and re-layouts, block_product(): blocks = panel.reshape(count_rows, -1, block)  29.2 us
    all_to_all x1, waiting for transfers between devices, copy_for_each(): lax.all_to_all(jnp.broadcast_to(shard[None], (devices, *shard.shape)), ax...  24.9 us
  transfers between devices with their start and end apart: 2, of which 2 were waited for; matrix products, arithmetic and copies ran while one was open for 0% of the time, Pallas kernels for 0%

profile of v1, /device:TPU:1, one launch (start us, length us, event | category | flops | bytes accessed | tf_op | source)
XLA Modules:
  0.0 811.0 jit_solution(1895617640428919213)
XLA Ops:
  1.7 23.5 %all_to_all.56 = f32[8,5,2048]{2,1,0:T(8,128)S(1)} all-to-all(f32[8,5,2048]{2,1,0:T(8,128)S(1)} %broadcast_in_dim.20), channel_id=1, replica_groups=mesh['row'=16,'col'=4,'cuts'=8] {'cuts'}, dimensions={0} | all-to-all | bytes 655360 | tf_op jit(solution)/shard_map/all_to_all | solution.py:9
  26.0 4.0 stack.6
  29.9 13.0 %all-to-all-start.1 = ((f32[16,40,2048]{2,1,0:T(8,128)}), f32[16,40,2048]{2,1,0:T(8,128)}, u32[]{:S(2)}, u32[]{:S(2)}) async-start(f32[16,40,2048]{2,1,0:T(8,128)} %stack.6), calls=%async_computation.1 | async-start | bytes 10485760 | tf_op jit(solution)/shard_map/all_to_all | solution.py:59
  43.0 233.6 %all-to-all-done.1 = f32[16,40,2048]{2,1,0:T(8,128)} async-done(((f32[16,40,2048]{2,1,0:T(8,128)}), f32[16,40,2048]{2,1,0:T(8,128)}, u32[]{:S(2)}, u32[]{:S(2)}) %all-to-all-start.1) | async-done | bytes 5242912 | tf_op jit(solution)/shard_map/all_to_all | solution.py:59
  276.6 7.9 copy.37
  284.4 6.7 reshape_reshape.12
  291.2 7.9 copy.38
  299.0 4.0 gather_fusion
  303.0 6.9 convolution_bitcast_fusion.3
  311.8 2.7 reshape_reshape.13
  316.5 17.4 %all_to_all.57 = f32[4,40,2048]{2,1,0:T(8,128)} all-to-all(f32[4,40,2048]{2,1,0:T(8,128)S(1)} %bitcast.48), channel_id=1, replica_groups=mesh['row'=16,'col'=4,'cuts'=8] {'col'}, dimensions={0} | all-to-all | bytes 2621440 | tf_op jit(solution)/shard_map/all_to_all | solution.py:33
  333.9 2.2 reduce_sum.56
  337.1 22.8 %all_to_all.58 = f32[8,5,2048]{2,1,0:T(8,128)} all-to-all(f32[8,5,2048]{2,1,0:T(8,128)S(1)} %reshape.45), channel_id=1, replica_groups=mesh['row'=16,'col'=4,'cuts'=8] {'cuts'}, dimensions={0} | all-to-all | bytes 655360 | tf_op jit(solution)/shard_map/all_to_all | solution.py:33
  361.0 18.4 %all_to_all.59 = f32[8,5,2048]{2,1,0:T(8,128)} all-to-all(f32[8,5,2048]{2,1,0:T(8,128)S(1)} %broadcast_in_dim.22), channel_id=1, replica_groups=mesh['row'=16,'col'=4,'cuts'=8] {'cuts'}, dimensions={0} | all-to-all | bytes 655360 | tf_op jit(solution)/shard_map/all_to_all | solution.py:9
  382.1 3.2 reshape.72
  385.2 13.9 %all-to-all-start.5 = ((f32[64,1,1600]{2,1,0:T(1,128)}), f32[64,1,1600]{2,1,0:T(1,128)}, u32[]{:S(2)}, u32[]{:S(2)}) async-start(f32[64,1,1600]{2,1,0:T(1,128)} %reshape.72), calls=%async_computation.5 | async-start | bytes 851968 | tf_op jit(solution)/shard_map/all_to_all | solution.py:9
  399.2 24.9 %all-to-all-done.5 = f32[64,1,1600]{2,1,0:T(1,128)} async-done(((f32[64,1,1600]{2,1,0:T(1,128)}), f32[64,1,1600]{2,1,0:T(1,128)}, u32[]{:S(2)}, u32[]{:S(2)}) %all-to-all-start.5) | async-done | bytes 409632 | tf_op jit(solution)/shard_map/all_to_all | solution.py:9
  424.6 3.4 reduce.6
  428.1 2.6 reshape.73
  432.2 3.6 cholesky.17
  437.2 3.1 custom-call.6
  440.8 22.9 %all_to_all.60 = f32[8,5,2048]{2,1,0:T(8,128)} all-to-all(f32[8,5,2048]{2,1,0:T(8,128)S(1)} %broadcast_in_dim.24), channel_id=1, replica_groups=mesh['row'=16,'col'=4,'cuts'=8] {'cuts'}, dimensions={0} | all-to-all | bytes 655360 | tf_op jit(solution)/shard_map/all_to_all | solution.py:9
  465.5 236.7 %all_to_all.61 = f32[16,40,2048]{2,1,0:T(8,128)S(1)} all-to-all(f32[16,40,2048]{2,1,0:T(8,128)S(1)} %stack.7), channel_id=1, replica_groups=mesh['row'=16,'col'=4,'cuts'=8] {'row'}, dimensions={0} | all-to-all | bytes 10485760 | tf_op jit(solution)/shard_map/all_to_all | solution.py:59
  702.2 5.4 copy.43
  707.6 6.7 reshape_reshape.14
  714.3 7.9 copy.44
  722.2 4.0 gather_fusion.1
  726.2 6.9 convolution_bitcast_fusion.2
  734.9 2.7 reshape_reshape.15
  739.7 18.7 %all_to_all.62 = f32[4,40,2048]{2,1,0:T(8,128)} all-to-all(f32[4,40,2048]{2,1,0:T(8,128)S(1)} %bitcast.49), channel_id=1, replica_groups=mesh['row'=16,'col'=4,'cuts'=8] {'col'}, dimensions={0} | all-to-all | bytes 2621440 | tf_op jit(solution)/shard_map/all_to_all | solution.py:33
  760.6 21.7 %all_to_all.63 = f32[8,5,2048]{2,1,0:T(8,128)} all-to-all(f32[8,5,2048]{2,1,0:T(8,128)} %reshape.48), channel_id=1, replica_groups=mesh['row'=16,'col'=4,'cuts'=8] {'cuts'}, dimensions={0} | all-to-all | bytes 655360 | tf_op jit(solution)/shard_map/all_to_all | solution.py:33
  784.0 25.1 %all_to_all.64 = f32[64,1,200]{2,1,0:T(1,128)S(1)} all-to-all(f32[64,1,200]{2,1,0:T(1,128)S(1)} %reshape.74), channel_id=1, replica_groups=mesh['row'=16,'col'=4,'cuts'=8] {'row','col'}, dimensions={0} | all-to-all | bytes 102400 | tf_op jit(solution)/shard_map/all_to_all | solution.py:9
  (45 shorter events, 26.0 us)
Async XLA Ops:
  0.6 302.4 %copy-start = (f32[43,128,128]{2,1,0:T(8,128)S(1)}, f32[43,128,128]{2,1,0:T(8,128)}, u32[]{:S(2)}) copy-start(f32[43,128,128]{2,1,0:T(8,128)} %param.7) | copy-start | bytes 8454148
  29.9 13.0 %copy-start.2 = (s32[43]{0:T(128)S(1)}, s32[43]{0:T(128)}, u32[]{:S(2)}) copy-start(s32[43]{0:T(128)} %param.9) | copy-start | bytes 520
  29.9 13.0 %copy-start.3 = (s32[43]{0:T(128)S(1)}, s32[43]{0:T(128)}, u32[]{:S(2)}) copy-start(s32[43]{0:T(128)} %param.8) | copy-start | bytes 520
  29.9 246.6 %all-to-all-start.1 = ((f32[16,40,2048]{2,1,0:T(8,128)}), f32[16,40,2048]{2,1,0:T(8,128)}, u32[]{:S(2)}, u32[]{:S(2)}) async-start(f32[16,40,2048]{2,1,0:T(8,128)} %stack.6), calls=%async_computation.1 | async-start | bytes 10485760 | tf_op jit(solution)/shard_map/all_to_all | solution.py:59
  385.2 38.9 %all-to-all-start.5 = ((f32[64,1,1600]{2,1,0:T(1,128)}), f32[64,1,1600]{2,1,0:T(1,128)}, u32[]{:S(2)}, u32[]{:S(2)}) async-start(f32[64,1,1600]{2,1,0:T(1,128)} %reshape.72), calls=%async_computation.5 | async-start | bytes 851968 | tf_op jit(solution)/shard_map/all_to_all | solution.py:9
  440.8 24.7 %copy-start.1 = (f32[5,2048]{1,0:T(8,128)}, f32[5,2048]{1,0:T(8,128)S(1)}, u32[]{:S(2)}) copy-start(f32[5,2048]{1,0:T(8,128)S(1)} %fusion.20) | copy-start | bytes 122884
